TPU v7x, 32 devices: a whole 2x2x4 slice. The times are simulated.
32 devices in a mesh: mem: 8 (over y, x, core), lat: 4 (over z).
Axes of the slice: x: 2, y: 2, z: 4, core: 2. Of those that a mesh axis runs over, the one named last changes fastest.
Arguments:
- state: float32 [8, 641, 8, 160], P('mem', None, 'lat'), may hold values from -6 to 6
- conv_kernel: float32 [25, 641], replicated, may hold values from -1.25 to 1.25
- norm_gain: float32 [641], replicated, may hold values from 0.5 to 1.5
- up_weight: bfloat16 [641, 1282], replicated, may hold values from -0.25 to 0.25
- down_weight: bfloat16 [1282, 641], replicated, may hold values from -0.15625 to 0.15625
- field_head_weight: bfloat16 [641, 72], replicated, may hold values from -0.25 to 0.25
- target: float32 [72, 8, 160], P(None, 'lat'), may hold values from -9 to 9
- field_weight: float32 [72], replicated, may hold values from 0.3 to 3
Outputs:
- loss: float32 [], replicated
- grad_kernel: float32 [25, 641], replicated
- grad_gain: float32 [641], replicated
- grad_up: float32 [641, 1282], replicated
- grad_down: float32 [1282, 641], replicated
- grad_head: float32 [641, 72], replicated
All inputs are finite; a program needn't handle non-finite values.
Results may differ from a plain program's by a relative error of at most 0.005.
The roundings to bfloat16 on the way count: a program that leaves them out, or rounds other values in their place, can miss the bound.
Values may be sent and summed in bfloat16 or wider, within the bound.
No kernel may reach another device: no remote copies, remote signals or barrier semaphores. Data moves between devices by JAX's collectives and lax.ppermute only.
A program may use at most 128 MiB of HBM per device.

v0:
```python
import math
import jax
import jax.numpy as jnp
from jax import lax
from jax.sharding import PartitionSpec as P

DELTA = 0.1
EPSILON = 1e-05


def extended(cells, sides, width):
    for axis, dim in sides:
        count = lax.axis_size(axis)
        ends = count - 1
        head = lax.slice_in_dim(cells, 0, width, axis=dim)
        tail = lax.slice_in_dim(cells, cells.shape[dim] - width, cells.shape[dim], axis=dim)
        cells = jnp.concatenate(
            [
                lax.ppermute(tail, axis, [(i, (i + 1) % count) for i in range(ends)]),
                cells,
                lax.ppermute(head, axis, [((i + 1) % count, i) for i in range(ends)]),
            ],
            axis=dim,
        )
    return cells


def softened_absolute(diff):
    return jnp.sqrt(diff * diff + DELTA * DELTA) - DELTA


def softened_derivative(diff):
    return diff / jnp.sqrt(diff * diff + DELTA * DELTA)


def gelu_parts(before_activation):
    cumul = 0.5 * (1.0 + jax.scipy.special.erf(before_activation / math.sqrt(2.0)))
    density = jnp.exp(-0.5 * before_activation * before_activation) / math.sqrt(2.0 * math.pi)
    return (before_activation * cumul, cumul + before_activation * density)


def leading_product(left, right):
    return lax.dot_general(
        left, right, (((0,), (0,)), ((), ())), preferred_element_type=jnp.float32
    )


def tail_dot(left, right):
    return lax.dot_general(
        left, right, (((1,), (1,)), ((), ())), preferred_element_type=jnp.float32
    )


def stencil(window, kernel, height):
    result = jnp.zeros((window.shape[0], height, window.shape[2]), jnp.float32)
    for col_off in range(5):
        shifted = jnp.roll(window, 2 - col_off, axis=2)
        for row_off in range(5):
            result = (
                result
                + kernel[row_off * 5 + col_off][:, None, None]
                * shifted[:, row_off : row_off + height]
            )
    return result


def kernel_grad(window, upstream, height):
    terms = [None] * 25
    for col_off in range(5):
        shifted = jnp.roll(window, 2 - col_off, axis=2)
        for row_off in range(5):
            terms[row_off * 5 + col_off] = jnp.sum(
                upstream * shifted[:, row_off : row_off + height], axis=(1, 2)
            )
    return jnp.stack(terms)


def forward_apply(field, window, kernel, gain, up_weight, down_weight, field_head_weight):
    height = field.shape[1]
    channels = field.shape[0]
    summed = (field + stencil(window, kernel, height)).reshape(channels, -1)
    center = summed - jnp.mean(summed, axis=0)
    inverse_norm = lax.rsqrt(jnp.mean(center * center, axis=0) + EPSILON)
    normalized_input = center * inverse_norm
    gain_scaled = (normalized_input * gain[:, None]).astype(jnp.bfloat16)
    before_activation = leading_product(up_weight, gain_scaled)
    activ, unused = gelu_parts(before_activation)
    hidden_activation = activ.astype(jnp.bfloat16)
    output = summed + leading_product(down_weight, hidden_activation)
    rounded_values = output.astype(jnp.bfloat16)
    member_prediction = leading_product(field_head_weight, rounded_values)
    return (
        member_prediction,
        (
            normalized_input,
            inverse_norm,
            gain_scaled,
            before_activation,
            hidden_activation,
            rounded_values,
        ),
    )


def backward(window, stored_residuals, cotangent, gain, up_weight, down_weight, field_head_weight):
    (
        normalized_input,
        inverse_norm,
        gain_scaled,
        before_activation,
        hidden_activation,
        rounded_values,
    ) = stored_residuals
    height = window.shape[1] - 4
    grad_head = tail_dot(rounded_values, cotangent)
    d_output = jnp.dot(field_head_weight, cotangent, preferred_element_type=jnp.float32)
    d_round = d_output.astype(jnp.bfloat16)
    grad_down = tail_dot(hidden_activation, d_round)
    d_hidden = jnp.dot(down_weight, d_round, preferred_element_type=jnp.float32)
    unused, slope = gelu_parts(before_activation)
    d_preact = (d_hidden * slope).astype(jnp.bfloat16)
    grad_up = tail_dot(gain_scaled, d_preact)
    d_scaled = jnp.dot(up_weight, d_preact, preferred_element_type=jnp.float32)
    grad_gain = jnp.sum(d_scaled * normalized_input, axis=1)
    d_normed = d_scaled * gain[:, None]
    d_summed = d_output + inverse_norm * (
        d_normed
        - jnp.mean(d_normed, axis=0)
        - normalized_input * jnp.mean(d_normed * normalized_input, axis=0)
    )
    upstream = d_summed.reshape(window.shape[0], height, window.shape[2])
    grad_kernel = kernel_grad(window, upstream, height)
    return (grad_kernel, grad_gain, grad_up, grad_down, grad_head)


def local(
    state, conv_kernel, norm_gain, up_weight, down_weight, field_head_weight, target, field_weight
):
    field = state[0]
    member_states = lax.axis_size("mem")
    height = field.shape[1]
    nlat = lax.axis_size("lat") * height
    width = field.shape[2]
    nfields = target.shape[0]
    window = extended(field, (("lat", 1),), 2)
    member_prediction, stored_residuals = forward_apply(
        field, window, conv_kernel, norm_gain, up_weight, down_weight, field_head_weight
    )
    grid_cell_values = member_prediction.shape[1]
    observed_target = target.reshape(nfields, grid_cell_values)
    row_float = (lax.axis_index("lat") * height + jnp.arange(height)).astype(jnp.float32)
    area_rows = jnp.cos(0.5 * math.pi * ((row_float + 0.5) / nlat - 1.0))
    area = jnp.repeat(area_rows, width)
    member_count = nlat * width * nfields
    scale_grad = 1.0 / (member_states * math.sqrt(member_count))
    pair_norm = 2.0 * member_states * (member_states - 1)
    block = grid_cell_values // member_states
    outgoing = member_prediction.reshape(1, nfields, member_states, block)
    gathered_members = lax.all_to_all(
        outgoing, "mem", split_axis=2, concat_axis=0, tiled=True
    ).reshape(member_states, nfields, block)
    mine = lax.axis_index("mem")
    truth_block = lax.dynamic_index_in_dim(
        observed_target.reshape(nfields, member_states, block), mine, 1, keepdims=False
    )
    area_block = lax.dynamic_index_in_dim(
        area.reshape(member_states, block), mine, 0, keepdims=False
    )
    differences = gathered_members[:, None] - gathered_members[None]
    ensemble_spread = (
        jnp.mean(softened_absolute(gathered_members - truth_block[None]), axis=0)
        - jnp.sum(softened_absolute(differences), axis=(0, 1)) / pair_norm
    )
    partial_value = jnp.sum(field_weight[:, None] * area_block[None, :] * ensemble_spread)
    loss = lax.psum(partial_value, ("mem", "lat")) / member_count
    pairwise_derivatives = jnp.sum(softened_derivative(differences), axis=1)
    member_cot = (
        field_weight[None, :, None]
        * area_block[None, None, :]
        * (
            softened_derivative(gathered_members - truth_block[None])
            - pairwise_derivatives / (member_states - 1)
        )
        * scale_grad
    )
    cot_rounded = member_cot.astype(jnp.bfloat16).reshape(member_states, nfields, 1, block)
    returned = lax.all_to_all(cot_rounded, "mem", split_axis=0, concat_axis=2, tiled=True)
    cotangent = returned.reshape(nfields, grid_cell_values)
    grads = backward(
        window, stored_residuals, cotangent, norm_gain, up_weight, down_weight, field_head_weight
    )
    totals = lax.psum((grads[0], grads[1], grads[2], grads[3], grads[4]), ("mem", "lat"))
    return (loss, totals[0], totals[1], totals[2], totals[3], totals[4])


def solution(mesh):
    return jax.shard_map(
        local,
        mesh=mesh,
        in_specs=(P("mem", None, "lat", None), P(), P(), P(), P(), P(), P(None, "lat", None), P()),
        out_specs=(P(), P(), P(), P(), P(), P()),
        check_vma=False,
    )
```

profile of v0, /device:TPU:0, one launch (start us, length us, event | category | flops | bytes accessed | tf_op | source)
XLA Modules:
  0.0 276.3 jit_solution(5404244537747198390)
XLA Ops:
  7.2 1.4 collective-permute-start.1
  8.6 6.6 %collective-permute-start = (f32[641,2,160]{0,2,1:T(8,128)}, f32[641,2,160]{0,2,1:T(8,128)}, u32[]{:S(2)}, u32[]{:S(2)}) collective-permute-start(f32[641,2,160]{0,2,1:T(8,128)} %bitcast.84), channel_id=1, source_target_pairs={{0,1},{1,2},{2,3},{4,5},{5,6},{6,7},{8,9},{9,10},{10,11},{12,13},{... | collective-permute-start | bytes 2461448 | tf_op jit(solution)/shard_map/ppermute | solution.py:19
  15.2 1.7 copy.28
  18.5 1.5 slice_reduce_fusion.24
  21.4 12.9 %collective-permute-done.1 = f32[641,2,160]{0,2,1:T(8,128)S(1)} collective-permute-done((f32[641,2,160]{0,2,1:T(8,128)}, f32[641,2,160]{0,2,1:T(8,128)S(1)}, u32[]{:S(2)}, u32[]{:S(2)}) %collective-permute-start.1) | collective-permute-done | bytes 820512 | tf_op jit(solution)/shard_map/ppermute | solution.py:21
  35.5 1.8 pad_maximum_fusion.8
  37.4 2.1 fusion.28
  39.5 3.0 %fusion.29 = (f32[641,6,159]{0,2,1:T(8,128)}, f32[641,6,159]{0,2,1:T(8,128)}) fusion(f32[641,6,160]{0,2,1:T(8,128)S(1)} %pad_maximum_fusion.8), kind=kLoop, calls=%fused_computation.120 | loop fusion | bytes 9784224 | tf_op jit(solution)/shard_map/jit(_roll_static)/slice | solution.py:57
  42.5 4.6 %fusion.3 = (f32[641,6,160]{0,2,1:T(8,128)S(1)}, f32[641,6,160]{0,2,1:T(8,128)S(1)}, f32[641,6,160]{0,2,1:T(8,128)S(1)}, f32[641,6,160]{0,2,1:T(8,128)S(1)}) fusion(f32[641,2,160]{0,2,1:T(8,128)S(1)} %copy-done.13, f32[641,2,160]{0,2,1:T(8,128)S(1)} %bitcast.86, f32[641,2,160]{0,2,1:T(8,128)} %collective-permute-done, ...), kind=kLoop, calls=%fused_computation.10 | loop fusion | flops 7384320 | bytes 22060656 | tf_op jit(solution)/shard_map/jit(_roll_static)/concatenate | solution.py:57
  47.2 5.9 %fusion.27 = (f32[2,160]{1,0:T(2,128)S(1)}, f32[641,2,160]{0,2,1:T(8,128)}) fusion(f32[641,2,160]{0,2,1:T(8,128)S(1)} %bitcast.87, f32[641,6,160]{0,2,1:T(8,128)S(1)} %get-tuple-element.86, f32[641]{0:T(1024)S(1)} %get-tuple-element.72, f32[641]{0:T(1024)S(1)} %get-tuple-element.73, f32[641]{0:T(1024)S(1)} %get-tuple-element.50, ...), kind=kLoop, calls=%fused_computation.118 | loop fusion | flops 10871040 | bytes 19756900 | tf_op jit(solution)/shard_map/reduce_sum | solution.py:82
  53.3 1.5 multiply_reduce_fusion.26
  56.3 2.2 multiply_convert_fusion
  60.9 3.9 %all-to-all-start = ((f32[1,72,8,40]{1,3,0,2:T(8,128)}), f32[1,72,8,40]{1,3,0,2:T(8,128)S(1)}, u32[]{:S(2)}, u32[]{:S(2)}) async-start(f32[1,72,8,40]{1,3,0,2:T(8,128)} %bitcast.95), calls=%async_computation | async-start | bytes 327680 | tf_op jit(solution)/shard_map/all_to_all | solution.py:159
  65.6 5.1 %all-to-all-done = f32[1,72,8,40]{1,3,0,2:T(8,128)S(1)} async-done(((f32[1,72,8,40]{1,3,0,2:T(8,128)}), f32[1,72,8,40]{1,3,0,2:T(8,128)S(1)}, u32[]{:S(2)}, u32[]{:S(2)}) %all-to-all-start) | async-done | bytes 92192 | tf_op jit(solution)/shard_map/all_to_all | solution.py:159
  71.5 7.5 %all_to_all.30 = bf16[8,72,1,40]{1,3,2,0:T(8,128)(2,1)S(1)} all-to-all(bf16[8,72,1,40]{1,3,2,0:T(8,128)(2,1)S(1)} %fusion.26), channel_id=1, replica_groups=mesh['mem'=8,'lat'=4] {'mem'}, dimensions={0} | all-to-all | bytes 92160 | tf_op jit(solution)/shard_map/all_to_all | solution.py:187
  81.2 3.1 %fusion.19 = f32[1282,641]{0,1:T(8,128)} fusion(bf16[1282,320]{0,1:T(8,128)(2,1)S(1)} %copy-done.21, f32[641,320]{0,1:T(8,128)S(1)} %convolution_bitcast_fusion.3), kind=kOutput, calls=%fused_computation.74 | convolution fusion | flops 526132800 | bytes 4928008 | tf_op jit(solution)/shard_map/dot_general | solution.py:49
  86.4 3.1 %fusion.22 = f32[641,1282]{1,0:T(8,128)} fusion(bf16[1282,320]{0,1:T(8,128)(2,1)S(1)} %fusion.5, f32[641,320]{0,1:T(8,128)S(1)} %copy-done.18, f32[641]{0:T(1024)S(1)} %copy-done.25), kind=kOutput, calls=%fused_computation.77 | convolution fusion | flops 526337920 | bytes 4930572 | tf_op jit(solution)/shard_map/dot_general | solution.py:49
  90.2 2.8 %multiply_reduce_fusion = (f32[641]{0:T(1024)S(1)}, f32[320]{0:T(512)S(1)}, f32[320]{0:T(512)S(1)}, f32[641,320]{0,1:T(8,128)S(1)}) fusion(f32[641,320]{0,1:T(8,128)} %copy-done.17, f32[641]{0:T(1024)S(1)} %copy-done.25, bf16[1282,320]{0,1:T(8,128)(2,1)} %copy-done.22, bf16[641,1282]{1,0:T(8,128)(2,1)S(1)} %copy-done), kind=kOutput, calls=%fused_computation.43 | convolution fusion | flops 527157120 | bytes 4112652 | tf_op jit(solution)/shard_map/dot_general | solution.py:123
  95.6 1.8 copy-done.2
  98.6 2.6 multiply_reduce_fusion.1
  101.6 42.5 %all-reduce.6 = (f32[]{:T(128)}, f32[25,641]{1,0:T(8,128)}, f32[641]{0:T(1024)}) all-reduce(f32[]{:T(128)} %multiply_reduce_fusion.28, f32[25,641]{1,0:T(8,128)S(1)} %stack.103, f32[641]{0:T(1024)S(1)} %get-tuple-element.26), channel_id=1, replica_groups=mesh['mem'=8,'lat'=4] {'mem','lat'}, use_global_device_ids=true, to_apply=%region_5.6 | all-reduce | flops 16667 | bytes 133336 | tf_op jit(solution)/shard_map/psum | solution.py:175
  144.8 116.7 %all-reduce.5.cloned.1.call-done = (f32[641,1282]{1,0:T(8,128)}, f32[1282,641]{0,1:T(8,128)}, f32[641,72]{0,1:T(8,128)}) async-done(((f32[641,1282]{1,0:T(8,128)}, f32[1282,641]{0,1:T(8,128)}, f32[641,72]{0,1:T(8,128)}), (f32[641,1282]{1,0:T(8,128)}, f32[1282,641]{0,1:T(8,128)}, f32[641,72]{0,1:T(8,128)})) %all-reduce.5.cloned.1.call-update) | async-done | bytes 6758720 | tf_op jit(solution)/shard_map/psum | solution.py:192
  261.5 4.2 %copy.36 = f32[641,1282]{1,0:T(8,128)} copy(f32[641,1282]{1,0:T(8,128)} %get-tuple-element.100) | data formatting | bytes 6574096
  265.8 1.8 copy.37
  (112 shorter events, 19.6 us)
Async XLA Ops:
  7.2 49.1 %copy-start = (bf16[641,1282]{1,0:T(8,128)(2,1)S(1)}, bf16[641,1282]{1,0:T(8,128)(2,1)}, u32[]{:S(2)}) copy-start(bf16[641,1282]{1,0:T(8,128)(2,1)} %param.11) | copy-start | bytes 4930576
  7.2 27.1 %collective-permute-start.1 = (f32[641,2,160]{0,2,1:T(8,128)}, f32[641,2,160]{0,2,1:T(8,128)S(1)}, u32[]{:S(2)}, u32[]{:S(2)}) collective-permute-start(f32[641,2,160]{0,2,1:T(8,128)} %bitcast.83), channel_id=1, source_target_pairs={{1,0},{2,1},{3,2},{5,4},{6,5},{7,6},{9,8},{10,9},{11,10},{13,12},{... | collective-permute-start | bytes 2461448 | tf_op jit(solution)/shard_map/ppermute | solution.py:21
  8.6 26.9 %collective-permute-start = (f32[641,2,160]{0,2,1:T(8,128)}, f32[641,2,160]{0,2,1:T(8,128)}, u32[]{:S(2)}, u32[]{:S(2)}) collective-permute-start(f32[641,2,160]{0,2,1:T(8,128)} %bitcast.84), channel_id=1, source_target_pairs={{0,1},{1,2},{2,3},{4,5},{5,6},{6,7},{8,9},{9,10},{10,11},{12,13},{... | collective-permute-start | bytes 2461448 | tf_op jit(solution)/shard_map/ppermute | solution.py:19
  34.2 3.1 %copy-start.12 = (f32[641,2,160]{0,2,1:T(8,128)}, f32[641,2,160]{0,2,1:T(8,128)S(1)}, u32[]{:S(2)}) copy-start(f32[641,2,160]{0,2,1:T(8,128)S(1)} %collective-permute-done.1) | copy-start | bytes 2461444
  39.5 3.0 %copy-start.9 = (f32[1,641,2,160]{1,3,2,0:T(8,128)S(1)}, f32[1,641,2,160]{1,3,2,0:T(8,128)}, u32[]{:S(2)}) copy-start(f32[1,641,2,160]{1,3,2,0:T(8,128)} %param.8) | copy-start | bytes 2461444
  39.5 3.0 %copy-start.13 = (f32[641,2,160]{0,2,1:T(8,128)S(1)}, f32[641,2,160]{0,2,1:T(8,128)}, u32[]{:S(2)}) copy-start(f32[641,2,160]{0,2,1:T(8,128)} %copy-done.12) | copy-start | bytes 2461444
  47.2 6.0 %copy-start.1 = (f32[641,6,160]{0,2,1:T(8,128)}, f32[641,6,160]{0,2,1:T(8,128)S(1)}, u32[]{:S(2)}) copy-start(f32[641,6,160]{0,2,1:T(8,128)S(1)} %get-tuple-element.85) | copy-start | bytes 7384324
  47.2 6.0 %copy-start.3 = (f32[641,6,160]{0,2,1:T(8,128)}, f32[641,6,160]{0,2,1:T(8,128)S(1)}, u32[]{:S(2)}) copy-start(f32[641,6,160]{0,2,1:T(8,128)S(1)} %get-tuple-element.86) | copy-start | bytes 7384324
  47.2 6.0 %copy-start.5 = (f32[641,6,160]{0,2,1:T(8,128)}, f32[641,6,160]{0,2,1:T(8,128)S(1)}, u32[]{:S(2)}) copy-start(f32[641,6,160]{0,2,1:T(8,128)S(1)} %get-tuple-element.84) | copy-start | bytes 7384324
  47.2 6.0 %copy-start.7 = (f32[641,6,160]{0,2,1:T(8,128)}, f32[641,6,160]{0,2,1:T(8,128)S(1)}, u32[]{:S(2)}) copy-start(f32[641,6,160]{0,2,1:T(8,128)S(1)} %get-tuple-element.87) | copy-start | bytes 7384324
  53.2 3.1 %copy-start.25 = (f32[641]{0:T(1024)S(1)}, f32[641]{0:T(1024)}, u32[]{:S(2)}) copy-start(f32[641]{0:T(1024)} %param.10) | copy-start | bytes 7696
  60.9 9.7 %all-to-all-start = ((f32[1,72,8,40]{1,3,0,2:T(8,128)}), f32[1,72,8,40]{1,3,0,2:T(8,128)S(1)}, u32[]{:S(2)}, u32[]{:S(2)}) async-start(f32[1,72,8,40]{1,3,0,2:T(8,128)} %bitcast.95), calls=%async_computation | async-start | bytes 327680 | tf_op jit(solution)/shard_map/all_to_all | solution.py:159
  64.8 196.7 %all-reduce.5.cloned.1.call-start = ((), (), s32[]{:S(2)}) async-start(), calls=%async_computation.2 | async-start | bytes 15040512 | tf_op jit(solution)/shard_map/psum | solution.py:192
  70.7 10.5 %copy-start.21 = (bf16[1282,320]{0,1:T(8,128)(2,1)S(1)}, bf16[1282,320]{0,1:T(8,128)(2,1)}, u32[]{:S(2)}) copy-start(bf16[1282,320]{0,1:T(8,128)(2,1)} %copy-done.20) | copy-start | bytes 2461444
  80.2 4.1 %copy-start.15 = (f32[641,320]{0,1:T(8,128)}, f32[641,320]{0,1:T(8,128)S(1)}, u32[]{:S(2)}) copy-start(f32[641,320]{0,1:T(8,128)S(1)} %convolution_bitcast_fusion.3) | copy-start | bytes 2461444
  81.2 3.1 %copy-start.27 = (bf16[1282,641]{0,1:T(8,128)(2,1)S(1)}, bf16[1282,641]{0,1:T(8,128)(2,1)}, u32[]{:S(2)}) copy-start(bf16[1282,641]{0,1:T(8,128)(2,1)} %param.12) | copy-start | bytes 4930576
  81.2 3.1 %copy-start.28 = (f32[1282,320]{0,1:T(8,128)S(1)}, f32[1282,320]{0,1:T(8,128)}, u32[]{:S(2)}) copy-start(f32[1282,320]{0,1:T(8,128)} %get-tuple-element.93) | copy-start | bytes 4922884
  89.5 3.5 %copy-start.11 = (f32[641,2,160]{0,2,1:T(8,128)S(1)}, f32[641,2,160]{0,2,1:T(8,128)}, u32[]{:S(2)}) copy-start(f32[641,2,160]{0,2,1:T(8,128)} %get-tuple-element.83) | copy-start | bytes 2461444
  89.5 3.5 %copy-start.16 = (f32[641,320]{0,1:T(8,128)S(1)}, f32[641,320]{0,1:T(8,128)}, u32[]{:S(2)}) copy-start(f32[641,320]{0,1:T(8,128)} %copy-done.15) | copy-start | bytes 2461444
  90.2 3.3 %copy-start.8 = (f32[641,6,160]{0,2,1:T(8,128)S(1)}, f32[641,6,160]{0,2,1:T(8,128)}, u32[]{:S(2)}) copy-start(f32[641,6,160]{0,2,1:T(8,128)} %copy-done.7) | copy-start | bytes 7384324
  94.8 2.6 copy-start.2
  94.8 3.6 %copy-start.4 = (f32[641,6,160]{0,2,1:T(8,128)S(1)}, f32[641,6,160]{0,2,1:T(8,128)}, u32[]{:S(2)}) copy-start(f32[641,6,160]{0,2,1:T(8,128)} %copy-done.3) | copy-start | bytes 7384324
  94.8 3.8 %copy-start.14 = (f32[641,2,160]{0,2,1:T(8,128)S(1)}, f32[641,2,160]{0,2,1:T(8,128)}, u32[]{:S(2)}) copy-start(f32[641,2,160]{0,2,1:T(8,128)} %copy-done.12) | copy-start | bytes 2461444
  261.5 4.3 %copy-start.19 = (f32[1282,641]{0,1:T(8,128)S(1)}, f32[1282,641]{0,1:T(8,128)}, u32[]{:S(2)}) copy-start(f32[1282,641]{0,1:T(8,128)} %get-tuple-element.101) | copy-start | bytes 9861148
  (9 other events, 16.5 us)
Sparse Core Ops, SparseCore 0:
  89.6 171.8 all-reduce.4
where the time goes:
time: 277 us; the launch traced here: 276 us
  waiting for transfers between devices  136 us (49%)
  blocking collectives  50 us (18%)
  local copies, waits for them, and re-layouts  24.4 us (9%)
  other arithmetic  21.9 us (8%)
  between operations  16.3 us (6%)
  matrix products  15.7 us (6%)
  starting transfers between devices  11.9 us (4%)
    psum x1, waiting for transfers between devices, local(): lax.psum((grads[0], grads[1], grads[2], grads[3], grads[4]), ('mem', 'lat'))  117 us
    psum x1, blocking collectives, local(): loss = lax.psum(partial_value, ('mem', 'lat')) / member_count  42.5 us
    unnamed x62, local copies, waits for them, and re-layouts  14.2 us
    ppermute x1, waiting for transfers between devices, extended(): lax.ppermute(head, axis, [((i + 1) % count, i) for i in range(ends)])  12.9 us
    all_to_all x1, blocking collectives, local(): lax.all_to_all(cot_rounded, 'mem', split_axis=0, concat_axis=2, tiled=True)  7.49 us
    dot_general x3, matrix products, tail_dot(): lax.dot_general(left, right, (((1,), (1,)), ((), ())), preferred_element_...  7.14 us
    ppermute x1, starting transfers between devices, extended(): lax.ppermute(tail, axis, [(i, (i + 1) % count) for i in range(ends)])  6.55 us
    reduce_sum x1, other arithmetic, forward_apply(): center = summed - jnp.mean(summed, axis=0)  5.94 us
  transfers between devices with their start and end apart: 4, of which 4 were waited for; matrix products, arithmetic and copies ran while one was open for 5% of the time, Pallas kernels for 0%

commit v1 on v0

--- a/solution.py
+++ b/solution.py
@@ -189,7 +189,7 @@
     grads = backward(
         window, stored_residuals, cotangent, norm_gain, up_weight, down_weight, field_head_weight
     )
-    totals = lax.psum((grads[0], grads[1], grads[2], grads[3], grads[4]), ("mem", "lat"))
+    totals = lax.psum(lax.psum((grads[0], grads[1], grads[2], grads[3], grads[4]), "lat"), "mem")
     return (loss, totals[0], totals[1], totals[2], totals[3], totals[4])
 
 

time: 277 us -> 599 us (2.16)
  waiting for transfers between devices: 136 us -> 454 us
    psum x1 -> x4, waiting for transfers between devices: 117 us -> 435 us  [the longest x2 300 us: local(): lax.psum((grads[0], grads[1], grads[2], grads[3], grads[4]), 'lat')]
    unnamed x62 -> x68, local copies, waits for them, and re-layouts: 14.2 us -> 15.9 us
  transfers between devices with their start and end apart: 4 -> 7, of which waited for: 4 -> 7; matrix products, arithmetic and copies ran while one was open for 5% -> 1% of each run, Pallas kernels for 0% -> 0%
where the time goes in v1:
time: 599 us; the launch traced here: 598 us
  waiting for transfers between devices  454 us (76%)
  blocking collectives  46.7 us (8%)
  local copies, waits for them, and re-layouts  29.4 us (5%)
  other arithmetic  22.4 us (4%)
  matrix products  17.3 us (3%)
  between operations  16.1 us (3%)
  starting transfers between devices  12 us (2%)
    psum x2, waiting for transfers between devices, local(): lax.psum((grads[0], grads[1], grads[2], grads[3], grads[4]), 'lat')  300 us
    psum x2, waiting for transfers between devices, local(): lax.psum(lax.psum((grads[0], grads[1], grads[2], grads[3], grads[4]), 'la...  135 us
    psum x1, blocking collectives, local(): loss = lax.psum(partial_value, ('mem', 'lat')) / member_count  39.2 us
    unnamed x68, local copies, waits for them, and re-layouts  15.9 us
    ppermute x1, waiting for transfers between devices, extended(): lax.ppermute(head, axis, [((i + 1) % count, i) for i in range(ends)])  12.9 us
  transfers between devices with their start and end apart: 7, of which 7 were waited for; matrix products, arithmetic and copies ran while one was open for 1% of the time, Pallas kernels for 0%

profile of v1, /device:TPU:0, one launch (start us, length us, event | category | flops | bytes accessed | tf_op | source)
XLA Modules:
  0.0 598.2 jit_solution(2550002198743518884)
XLA Ops:
  8.6 6.6 %collective-permute-start = (f32[641,2,160]{0,2,1:T(8,128)}, f32[641,2,160]{0,2,1:T(8,128)}, u32[]{:S(2)}, u32[]{:S(2)}) collective-permute-start(f32[641,2,160]{0,2,1:T(8,128)} %bitcast.84), channel_id=1, source_target_pairs={{0,1},{1,2},{2,3},{4,5},{5,6},{6,7},{8,9},{9,10},{10,11},{12,13},{... | collective-permute-start | bytes 2461448 | tf_op jit(solution)/shard_map/ppermute | solution.py:19
  15.2 1.7 copy.28
  21.3 12.9 %collective-permute-done.1 = f32[641,2,160]{0,2,1:T(8,128)S(1)} collective-permute-done((f32[641,2,160]{0,2,1:T(8,128)}, f32[641,2,160]{0,2,1:T(8,128)S(1)}, u32[]{:S(2)}, u32[]{:S(2)}) %collective-permute-start.1) | collective-permute-done | bytes 820512 | tf_op jit(solution)/shard_map/ppermute | solution.py:21
  35.5 1.8 pad_maximum_fusion.8
  37.3 2.1 fusion.28
  39.5 3.0 fusion.29
  42.5 4.6 fusion.3
  47.2 5.9 fusion.27
  56.2 2.2 multiply_convert_fusion
  62.4 3.9 all-to-all-start
  67.1 5.1 all-to-all-done
  73.6 7.5 %all_to_all.30 = bf16[8,72,1,40]{1,3,2,0:T(8,128)(2,1)S(1)} all-to-all(bf16[8,72,1,40]{1,3,2,0:T(8,128)(2,1)S(1)} %fusion.26), channel_id=1, replica_groups=mesh['mem'=8,'lat'=4] {'mem'}, dimensions={0} | all-to-all | bytes 92160 | tf_op jit(solution)/shard_map/all_to_all | solution.py:187
  82.2 3.3 fusion.5
  87.2 3.1 fusion.22
  90.3 3.1 fusion.19
  98.1 2.5 multiply_reduce_fusion.1
  100.9 2.6 stack.103
  104.6 33.9 %all-reduce.13.cloned.1.call-done = (f32[25,641]{1,0:T(8,128)}, f32[641]{0:T(1024)}) async-done(((f32[25,641]{1,0:T(8,128)}, f32[641]{0:T(1024)}), (f32[25,641]{1,0:T(8,128)}, f32[641]{0:T(1024)})) %all-reduce.13.cloned.1.call-update) | async-done | bytes 66680 | tf_op jit(solution)/shard_map/psum | solution.py:192
  138.5 266.0 %all-reduce.15.cloned.1.call-done = (f32[641,1282]{1,0:T(8,128)}, f32[1282,641]{0,1:T(8,128)}, f32[641,72]{0,1:T(8,128)}) async-done(((f32[641,1282]{1,0:T(8,128)}, f32[1282,641]{0,1:T(8,128)}, f32[641,72]{0,1:T(8,128)}), (f32[641,1282]{1,0:T(8,128)}, f32[1282,641]{0,1:T(8,128)}, f32[641,72]{0,1:T(8,128)})) %all-reduce.15.cloned.1.call-update) | async-done | bytes 6758720 | tf_op jit(solution)/shard_map/psum | solution.py:192
  406.0 39.2 %psum.77 = f32[]{:T(128)} all-reduce(f32[]{:T(128)} %multiply_reduce_fusion.28), channel_id=1, replica_groups=mesh['mem'=8,'lat'=4] {'mem','lat'}, use_global_device_ids=true, to_apply=%region_5.6 | all-reduce | flops 1 | bytes 8 | tf_op jit(solution)/shard_map/psum | solution.py:175
  445.8 13.0 %all-reduce.9.cloned.1.call-done = (f32[25,641]{1,0:T(8,128)}, f32[641]{0:T(1024)}) async-done(((f32[25,641]{1,0:T(8,128)}, f32[641]{0:T(1024)}), (f32[25,641]{1,0:T(8,128)}, f32[641]{0:T(1024)})) %all-reduce.9.cloned.1.call-update) | async-done | bytes 66680 | tf_op jit(solution)/shard_map/psum | solution.py:192
  458.8 122.1 %all-reduce.11.cloned.1.call-done = (f32[641,1282]{1,0:T(8,128)}, f32[1282,641]{0,1:T(8,128)}, f32[641,72]{0,1:T(8,128)}) async-done(((f32[641,1282]{1,0:T(8,128)}, f32[1282,641]{0,1:T(8,128)}, f32[641,72]{0,1:T(8,128)}), (f32[641,1282]{1,0:T(8,128)}, f32[1282,641]{0,1:T(8,128)}, f32[641,72]{0,1:T(8,128)})) %all-reduce.11.cloned.1.call-update) | async-done | bytes 6758720 | tf_op jit(solution)/shard_map/psum | solution.py:192
  583.7 4.2 copy.42
  588.0 1.8 copy.43
  (127 shorter events, 30.1 us)
Async XLA Ops:
  7.2 49.0 %copy-start = (bf16[641,1282]{1,0:T(8,128)(2,1)S(1)}, bf16[641,1282]{1,0:T(8,128)(2,1)}, u32[]{:S(2)}) copy-start(bf16[641,1282]{1,0:T(8,128)(2,1)} %param.11) | copy-start | bytes 4930576
  7.2 27.1 %collective-permute-start.1 = (f32[641,2,160]{0,2,1:T(8,128)}, f32[641,2,160]{0,2,1:T(8,128)S(1)}, u32[]{:S(2)}, u32[]{:S(2)}) collective-permute-start(f32[641,2,160]{0,2,1:T(8,128)} %bitcast.83), channel_id=1, source_target_pairs={{1,0},{2,1},{3,2},{5,4},{6,5},{7,6},{9,8},{10,9},{11,10},{13,12},{... | collective-permute-start | bytes 2461448 | tf_op jit(solution)/shard_map/ppermute | solution.py:21
  8.6 26.9 %collective-permute-start = (f32[641,2,160]{0,2,1:T(8,128)}, f32[641,2,160]{0,2,1:T(8,128)}, u32[]{:S(2)}, u32[]{:S(2)}) collective-permute-start(f32[641,2,160]{0,2,1:T(8,128)} %bitcast.84), channel_id=1, source_target_pairs={{0,1},{1,2},{2,3},{4,5},{5,6},{6,7},{8,9},{9,10},{10,11},{12,13},{... | collective-permute-start | bytes 2461448 | tf_op jit(solution)/shard_map/ppermute | solution.py:19
  21.3 52.2 %copy-start.28 = (f32[72]{0:T(128)}, f32[72]{0:T(128)S(1)}, u32[]{:S(2)}) copy-start(f32[72]{0:T(128)S(1)} %broadcast_multiply_fusion.3) | copy-start | bytes 868
  34.2 3.1 copy-start.12
  39.5 3.0 copy-start.9
  39.5 3.0 copy-start.13
  47.1 6.0 copy-start.1
  47.1 6.0 copy-start.3
  47.1 6.0 copy-start.5
  47.2 6.0 copy-start.7
  53.1 3.1 copy-start.24
  62.4 9.7 %all-to-all-start = ((f32[1,72,8,40]{1,3,0,2:T(8,128)}), f32[1,72,8,40]{1,3,0,2:T(8,128)S(1)}, u32[]{:S(2)}, u32[]{:S(2)}) async-start(f32[1,72,8,40]{1,3,0,2:T(8,128)} %bitcast.95), calls=%async_computation | async-start | bytes 327680 | tf_op jit(solution)/shard_map/all_to_all | solution.py:159
  66.3 72.2 %all-reduce.13.cloned.1.call-start = ((), (), s32[]{:S(2)}) async-start(), calls=%async_computation.4 | async-start | bytes 204800 | tf_op jit(solution)/shard_map/psum | solution.py:192
  67.1 6.4 %copy-start.22 = (f32[72,40]{0,1:T(8,128)}, f32[72,40]{0,1:T(8,128)S(1)}, u32[]{:S(2)}) copy-start(f32[72,40]{0,1:T(8,128)S(1)} %dynamic-slice_bitcast_fusion) | copy-start | bytes 34564
  82.2 3.3 copy-start.16
  87.2 3.1 copy-start.19
  90.2 3.1 copy-start.11
  90.3 3.1 copy-start.27
  90.3 3.5 copy-start.8
  103.5 301.0 %all-reduce.15.cloned.1.call-start = ((), (), s32[]{:S(2)}) async-start(), calls=%async_computation.5 | async-start | bytes 15040512 | tf_op jit(solution)/shard_map/psum | solution.py:192
  104.5 354.3 %all-reduce.9.cloned.1.call-start = ((), (), s32[]{:S(2)}) async-start(), calls=%async_computation.2 | async-start | bytes 204800 | tf_op jit(solution)/shard_map/psum | solution.py:192
  138.5 442.4 %all-reduce.11.cloned.1.call-start = ((), (), s32[]{:S(2)}) async-start(), calls=%async_computation.3 | async-start | bytes 15040512 | tf_op jit(solution)/shard_map/psum | solution.py:192
  583.7 4.3 copy-start.17
  (14 other events, 24.7 us)
Sparse Core Ops, SparseCore 0:
  103.6 34.7 all-reduce.12
  141.6 262.8 all-reduce.14
  407.7 51.0 all-reduce.8
  462.3 118.5 all-reduce.10
